TPU v7x, 32 devices: a whole 2x2x4 slice. The times are simulated.
32 devices in a mesh: shard: 8 (over z, x), rep: 4 (over y, core).
Axes of the slice: x: 2, y: 2, z: 4, core: 2. Of those that a mesh axis runs over, the one named last changes fastest.
Arguments:
- lender_block: int32 [96, 8], P(('shard', 'rep')), may hold values from 0 to 255, as said below
- confidence: bfloat16 [96, 8, 256, 256], P(('shard', 'rep')), may hold values from 0 to 80, as said below
- lender_factors: bfloat16 [65536, 128], P('shard'), may hold values from -4 to 4
Outputs:
- borrower_factors: float32 [24576, 128], P(('shard', 'rep'))
- lender_rhs: float32 [65536, 128], P('shard')
Inputs may be any that keep to these rules, and one draw needn't show every extreme that they name: `lender_block`: within one device's 3 borrower blocks, at most 6 of the 3 x 8 entries name blocks of any one owner (block // 32), and on every device some owner is named exactly 6 times. `confidence`: about half the entries are zero; the others are positive.
All inputs are finite; a program needn't handle non-finite values.
Results may differ from a plain program's by a relative error of at most 0.0047.
Values may be sent and summed in bfloat16 or wider, within the bound.
A program may use at most 128 MiB of HBM per device.

v0:
```python
import jax
import jax.numpy as jnp
from jax import lax
from jax.sharding import PartitionSpec as P

CG_STEPS = 3
HIGH = lax.Precision.HIGHEST


def apply_system(direction, confidence, fetched, gram):
    low = direction.astype(jnp.bfloat16)
    scores = jnp.einsum("btr,bklr->bktl", low, fetched, preferred_element_type=jnp.float32)
    weighted = (confidence.astype(jnp.float32) * scores).astype(jnp.bfloat16)
    back = jnp.einsum("bktl,bklr->btr", weighted, fetched, preferred_element_type=jnp.float32)
    width = direction.shape[-1]
    global_part = jnp.dot(
        direction.reshape(-1, width), gram, precision=HIGH, preferred_element_type=jnp.float32
    )
    return global_part.reshape(direction.shape) + 0.1 * direction + back


def per_device(lender_block, confidence, lender_factors):
    shards = lax.axis_size("shard")
    blocks, lists = lender_block.shape
    tile = confidence.shape[2]
    rank = lender_factors.shape[1]
    owned = lender_factors.shape[0] // tile
    entries = blocks * lists
    slots = (2 * entries + shards - 1) // shards
    local_gram = lax.dot_general(
        lender_factors, lender_factors, (((0,), (0,)), ((), ())), preferred_element_type=jnp.float32
    )
    gram = lax.psum(local_gram, "shard")
    flat = lender_block.reshape(entries)
    owner = flat // owned
    within = flat - owner * owned
    member = (owner[:, None] == jnp.arange(shards, dtype=jnp.int32)[None, :]).astype(jnp.int32)
    position = jnp.sum(jnp.cumsum(member, axis=0) * member, axis=1) - 1
    slot_index = owner * slots + position
    requests = (
        jnp.zeros((shards * slots,), jnp.int32).at[slot_index].set(within).reshape(shards, slots)
    )
    table = lender_factors.reshape(owned, tile, rank)
    incoming = lax.all_to_all(requests, "shard", split_axis=0, concat_axis=0, tiled=True)
    replies = lax.all_to_all(table[incoming], "shard", split_axis=0, concat_axis=0, tiled=True)
    fetched = replies.reshape(shards * slots, tile, rank)[slot_index].reshape(
        blocks, lists, tile, rank
    )
    rhs = jnp.einsum("bktl,bklr->btr", confidence, fetched, preferred_element_type=jnp.float32)
    solution = jnp.zeros_like(rhs)
    resid = rhs
    direction = rhs
    norm_now = jnp.sum(resid * resid, axis=2, keepdims=True)
    for count in range(CG_STEPS):
        image = apply_system(direction, confidence, fetched, gram)
        alpha = norm_now / (jnp.sum(direction * image, axis=2, keepdims=True) + 1e-06)
        solution = solution + alpha * direction
        resid = resid - alpha * image
        norm_next = jnp.sum(resid * resid, axis=2, keepdims=True)
        direction = resid + norm_next / (norm_now + 1e-06) * direction
        norm_now = norm_next
    solved = solution.astype(jnp.bfloat16)
    partial_rhs = jnp.einsum(
        "bktl,btr->bklr", confidence, solved, preferred_element_type=jnp.float32
    )
    outgoing = (
        jnp.zeros((shards * slots, tile, rank), jnp.float32)
        .at[slot_index]
        .set(partial_rhs.reshape(entries, tile, rank))
    )
    returned = lax.all_to_all(
        outgoing.reshape(shards, slots, tile, rank),
        "shard",
        split_axis=0,
        concat_axis=0,
        tiled=True,
    )
    selector = (
        incoming.reshape(-1)[None, :] == jnp.arange(owned, dtype=jnp.int32)[:, None]
    ).astype(jnp.float32)
    owner_sum = jnp.dot(
        selector,
        returned.reshape(shards * slots, tile * rank),
        precision=HIGH,
        preferred_element_type=jnp.float32,
    )
    total = lax.psum(owner_sum, "rep")
    lenders_all = owned * tile * shards
    lender_rhs = total.reshape(owned * tile, rank) / lenders_all
    return (solution.reshape(blocks * tile, rank), lender_rhs)


def solution(mesh):
    in_specs = (P(("shard", "rep"), None), P(("shard", "rep"), None, None, None), P("shard", None))
    out_specs = (P(("shard", "rep"), None), P("shard", None))
    return jax.shard_map(
        per_device, mesh=mesh, in_specs=in_specs, out_specs=out_specs, check_vma=False
    )
```

profile of v0, /device:TPU:0, one launch (start us, length us, event | category | flops | bytes accessed | tf_op | source)
XLA Modules:
  0.0 416.2 jit_solution(9014133852448018927)
XLA Ops:
  7.2 0.0 copy-start
  7.2 0.9 reshape.224
  8.1 0.8 reshape.223
  8.9 0.1 fusion.50
  9.0 0.2 select_reduce_fusion
  9.2 0.6 scatter_custom_fusion
  9.8 0.1 all_to_all.14
  9.9 13.6 %all_to_all.22 = s32[8,1,6]{2,1,0:T(1,128)S(1)} all-to-all(s32[8,1,6]{2,1,0:T(1,128)S(1)} %bitcast.112), channel_id=1, replica_groups=mesh['shard'=8,'rep'=4] {'shard'}, dimensions={0} | all-to-all | bytes 384 | tf_op jit(solution)/shard_map/all_to_all | solution.py:44
  23.5 0.1 copy.32
  23.6 0.1 copy.33
  23.7 0.1 reshape.233
  23.8 2.7 gather_fusion
  26.5 4.4 %all-to-all-start.1 = ((bf16[8,6,256,128]{3,2,1,0:T(8,128)(2,1)}), bf16[8,6,256,128]{3,2,1,0:T(8,128)(2,1)}, u32[]{:S(2)}, u32[]{:S(2)}) async-start(bf16[8,6,256,128]{3,2,1,0:T(8,128)(2,1)} %bitcast.106), calls=%async_computation.1 | async-start | bytes 6291456 | tf_op jit(solution)/shard_map/all_to_all | solution.py:45
  30.9 0.0 all-reduce.3.cloned.1.call-start
  31.0 1.4 fusion.55
  32.4 0.0 all-reduce.3.cloned.1.call-update
  32.4 4.7 %copy.37 = bf16[3,8,256,256]{2,3,1,0:T(8,128)(2,1)} copy(bf16[3,8,256,256]{3,2,1,0:T(8,128)(2,1)} %param.4) | data formatting | bytes 6291456 | tf_op args[1]
  37.1 64.9 %all-to-all-done.1 = bf16[8,6,256,128]{3,2,1,0:T(8,128)(2,1)} async-done(((bf16[8,6,256,128]{3,2,1,0:T(8,128)(2,1)}), bf16[8,6,256,128]{3,2,1,0:T(8,128)(2,1)}, u32[]{:S(2)}, u32[]{:S(2)}) %all-to-all-start.1) | async-done | bytes 3145760 | tf_op jit(solution)/shard_map/all_to_all | solution.py:45
  102.0 3.8 gather_fusion.1
  105.8 3.5 convolution_bitcast_fusion
  109.4 4.3 %fusion.18 = f32[3,256,128]{1,2,0:T(8,128)S(1)} fusion(bf16[3,8,256,128]{3,2,1,0:T(8,128)(2,1)} %bitcast.108, bf16[3,8,256,256]{2,3,1,0:T(8,128)(2,1)} %copy.37, f32[3,256,128]{1,2,0:T(8,128)S(1)} %convolution_bitcast_fusion), kind=kOutput, calls=%fused_computation.20 | convolution fusion | flops 810123264 | bytes 5505024 | tf_op jit(solution)/shard_map/bktl,bklr->btr/dot_general | solution.py:14
  113.7 13.5 %all-reduce.3.cloned.1.call-done = f32[128,128]{1,0:T(8,128)} async-done(((f32[128,128]{1,0:T(8,128)}), f32[128,128]{1,0:T(8,128)}) %all-reduce.3.cloned.1.call-update) | async-done | bytes 65552 | tf_op jit(solution)/shard_map/psum | solution.py:33
  127.2 1.4 multiply_reduce_fusion.3
  128.6 0.1 multiply_reduce_fusion.2
  128.7 0.1 multiply_add_fusion.2
  128.8 5.1 %fusion.21 = f32[3,256,128]{1,2,0:T(8,128)} fusion(bf16[3,8,256,128]{3,2,1,0:T(8,128)(2,1)} %bitcast.109, bf16[3,8,256,256]{2,3,1,0:T(8,128)(2,1)} %copy.37, f32[3,256,128]{1,2,0:T(8,128)S(1)} %multiply_add_fusion.2), kind=kOutput, calls=%fused_computation.21 | convolution fusion | flops 810123264 | bytes 5505024 | tf_op jit(solution)/shard_map/bktl,bklr->btr/dot_general | solution.py:14
  133.8 1.6 multiply_reduce_fusion.1
  135.4 0.1 multiply_reduce_fusion
  135.5 0.8 multiply_add_fusion.1
  136.3 5.2 %fusion.24 = f32[3,256,128]{1,2,0:T(8,128)} fusion(bf16[3,8,256,128]{3,2,1,0:T(8,128)(2,1)} %bitcast.110, bf16[3,8,256,256]{2,3,1,0:T(8,128)(2,1)} %copy.37, f32[3,256,128]{1,2,0:T(8,128)} %multiply_add_fusion.1), kind=kOutput, calls=%fused_computation.22 | convolution fusion | flops 810123264 | bytes 5505024 | tf_op jit(solution)/shard_map/bktl,bklr->btr/dot_general | solution.py:14
  141.5 1.6 fusion.31
  143.1 1.1 multiply_add_fusion
  144.2 4.1 fusion.38
  148.3 3.6 copy.52
  151.9 3.4 broadcast_in_dim.5
  155.3 7.9 %scatter_fusion = f32[48,256,128]{2,1,0:T(8,128)} fusion(f32[48,256,128]{2,1,0:T(8,128)} %broadcast_in_dim.5, s32[24]{0:T(128)S(1)} %fusion.52, f32[24,256,128]{2,1,0:T(8,128)} %copy.52), kind=kCustom, calls=%fused_computation.3 | custom fusion | bytes 9437280 | tf_op jit(solution)/shard_map/scatter | solution.py:69
  163.3 4.8 %all-to-all-start.2 = ((f32[8,6,256,128]{3,2,1,0:T(8,128)}), f32[8,6,256,128]{3,2,1,0:T(8,128)}, u32[]{:S(2)}, u32[]{:S(2)}) async-start(f32[8,6,256,128]{3,2,1,0:T(8,128)} %bitcast.104), calls=%async_computation.2 | async-start | bytes 12582912 | tf_op jit(solution)/shard_map/all_to_all | solution.py:71
  168.0 0.2 all-reduce.5.cloned.1.call-start
  168.2 0.5 broadcast.206
  168.8 0.7 reduce.3
  169.4 0.1 eq.31
  169.5 135.1 %all-to-all-done.2 = f32[8,6,256,128]{3,2,1,0:T(8,128)} async-done(((f32[8,6,256,128]{3,2,1,0:T(8,128)}), f32[8,6,256,128]{3,2,1,0:T(8,128)}, u32[]{:S(2)}, u32[]{:S(2)}) %all-to-all-start.2) | async-done | bytes 6291488 | tf_op jit(solution)/shard_map/all_to_all | solution.py:71
  304.6 10.8 %fusion.3 = f32[32,32768]{1,0:T(8,128)} fusion(f32[6,8,256,128]{3,2,1,0:T(8,128)} %bitcast.40, s32[48]{0:T(128)S(1)} %eq.31), kind=kOutput, calls=%fused_computation.10 | convolution fusion | flops 603981312 | bytes 10485952 | tf_op jit(solution)/shard_map/dot_general | solution.py:81
  315.4 0.0 all-reduce.5.cloned.1.call-update
  315.4 0.9 copy.51
  316.3 83.7 %all-reduce.5.cloned.1.call-done = f32[32,32768]{1,0:T(8,128)} async-done(((f32[32,32768]{1,0:T(8,128)}), f32[32,32768]{1,0:T(8,128)}) %all-reduce.5.cloned.1.call-update) | async-done | bytes 4194320 | tf_op jit(solution)/shard_map/psum | solution.py:87
  400.0 4.4 %broadcast_multiply_fusion = f32[32,32768]{1,0:T(8,128)} fusion(f32[32,32768]{1,0:T(8,128)} %all-reduce.5.cloned.1.call-done), kind=kLoop, calls=%fused_computation.19 | loop fusion | flops 1048576 | bytes 8388608 | tf_op jit(solution)/shard_map/div | solution.py:89
  404.5 4.9 %div.83 = f32[8192,128]{1,0:T(8,128)} reshape(f32[32,32768]{1,0:T(8,128)} %broadcast_multiply_fusion) | data formatting | bytes 8388608 | tf_op jit(solution)/shard_map/div | solution.py:89
  (16 shorter events, 0.1 us)
Async XLA Ops:
  7.2 16.6 %copy-start = (bf16[8192,128]{1,0:T(8,128)(2,1)S(1)}, bf16[8192,128]{1,0:T(8,128)(2,1)}, u32[]{:S(2)}) copy-start(bf16[8192,128]{1,0:T(8,128)(2,1)} %param.5) | copy-start | bytes 6291460
  26.5 75.5 %all-to-all-start.1 = ((bf16[8,6,256,128]{3,2,1,0:T(8,128)(2,1)}), bf16[8,6,256,128]{3,2,1,0:T(8,128)(2,1)}, u32[]{:S(2)}, u32[]{:S(2)}) async-start(bf16[8,6,256,128]{3,2,1,0:T(8,128)(2,1)} %bitcast.106), calls=%async_computation.1 | async-start | bytes 6291456 | tf_op jit(solution)/shard_map/all_to_all | solution.py:45
  30.9 96.2 %all-reduce.3.cloned.1.call-start = ((), (), s32[]{:S(2)}) async-start(), calls=%async_computation.3 | async-start | bytes 131072 | tf_op jit(solution)/shard_map/psum | solution.py:33
  128.7 5.1 %copy-start.2 = (f32[128,128]{1,0:T(8,128)S(1)}, f32[128,128]{1,0:T(8,128)}, u32[]{:S(2)}) copy-start(f32[128,128]{1,0:T(8,128)} %all-reduce.3.cloned.1.call-done) | copy-start | bytes 196612
  136.3 5.2 %copy-start.1 = (f32[3,256,128]{1,2,0:T(8,128)S(1)}, f32[3,256,128]{1,2,0:T(8,128)}, u32[]{:S(2)}) copy-start(f32[3,256,128]{1,2,0:T(8,128)} %multiply_add_fusion.1) | copy-start | bytes 1179652
  163.3 141.3 %all-to-all-start.2 = ((f32[8,6,256,128]{3,2,1,0:T(8,128)}), f32[8,6,256,128]{3,2,1,0:T(8,128)}, u32[]{:S(2)}, u32[]{:S(2)}) async-start(f32[8,6,256,128]{3,2,1,0:T(8,128)} %bitcast.104), calls=%async_computation.2 | async-start | bytes 12582912 | tf_op jit(solution)/shard_map/all_to_all | solution.py:71
  168.0 232.0 %all-reduce.5.cloned.1.call-start = ((), (), s32[]{:S(2)}) async-start(), calls=%async_computation.4 | async-start | bytes 8388608 | tf_op jit(solution)/shard_map/psum | solution.py:87
Sparse Core Ops, SparseCore 0:
  35.7 91.3 all-reduce.2
  315.5 84.4 all-reduce.4
where the time goes:
time: 417 us; the launch traced here: 416 us
  waiting for transfers between devices  297 us (71%)
  matrix products  39 us (9%)
  local copies, waits for them, and re-layouts  35.2 us (8%)
  between operations  14.2 us (3%)
  blocking collectives  13.6 us (3%)
  starting transfers between devices  9.46 us (2%)
  other arithmetic  7.59 us (2%)
    all_to_all x1, waiting for transfers between devices, per_device(): lax.all_to_all(outgoing.reshape(shards, slots, tile, rank), 'shard', spli...  135 us
    psum x1, waiting for transfers between devices, per_device(): total = lax.psum(owner_sum, 'rep')  83.7 us
    all_to_all x1, waiting for transfers between devices, per_device(): lax.all_to_all(table[incoming], 'shard', split_axis=0, concat_axis=0, til...  64.9 us
    dot_general x3, matrix products, apply_system(): jnp.einsum('bktl,bklr->btr', weighted, fetched, preferred_element_type=jn...  14.5 us
    all_to_all x1, blocking collectives, per_device(): lax.all_to_all(requests, 'shard', split_axis=0, concat_axis=0, tiled=True)  13.6 us
    psum x1, waiting for transfers between devices, per_device(): gram = lax.psum(local_gram, 'shard')  13.5 us
    dot_general x1, matrix products, per_device(): jnp.dot(selector, returned.reshape(shards * slots, tile * rank), precisio...  10.8 us
  transfers between devices with their start and end apart: 4, of which 4 were waited for; matrix products, arithmetic and copies ran while one was open for 5% of the time, Pallas kernels for 0%

commit v1 on v0

--- a/solution.py
+++ b/solution.py
@@ -2,6 +2,7 @@
 import jax.numpy as jnp
 from jax import lax
 from jax.sharding import PartitionSpec as P
+from jax.lax import all_gather
 
 CG_STEPS = 3
 HIGH = lax.Precision.HIGHEST
@@ -30,7 +31,7 @@
     local_gram = lax.dot_general(
         lender_factors, lender_factors, (((0,), (0,)), ((), ())), preferred_element_type=jnp.float32
     )
-    gram = lax.psum(local_gram, "shard")
+    gram = jnp.sum(all_gather(local_gram, axis_name="shard"), axis=0)
     flat = lender_block.reshape(entries)
     owner = flat // owned
     within = flat - owner * owned

time: 417 us -> 419 us (level)
  blocking collectives: 13.6 us -> 98.7 us
  waiting for transfers between devices: 297 us -> 216 us
    all_gather x0 -> x1, blocking collectives: none -> 85.2 us  [per_device(): gram = jnp.sum(all_gather(local_gram, axis_name='shard'), axis=0)]
    all_to_all x1, waiting for transfers between devices: 64.9 us -> 0.01 us  [per_device(): lax.all_to_all(table[incoming], 'shard', split_axis=0, concat_axis=0, til...]
    psum x1 -> x0, waiting for transfers between devices: 13.5 us -> none  [per_device(): gram = lax.psum(local_gram, 'shard')]
  transfers between devices with their start and end apart: 4 -> 3, of which waited for: 4 -> 2; matrix products, arithmetic and copies ran while one was open for 5% -> 2% of each run, Pallas kernels for 0% -> 0%
where the time goes in v1:
time: 419 us; the launch traced here: 418 us
  waiting for transfers between devices  216 us (52%)
  blocking collectives  98.7 us (24%)
  matrix products  37.5 us (9%)
  local copies, waits for them, and re-layouts  35.2 us (8%)
  between operations  14.2 us (3%)
  starting transfers between devices  9.42 us (2%)
  other arithmetic  7.62 us (2%)
    all_to_all x1, waiting for transfers between devices, per_device(): lax.all_to_all(outgoing.reshape(shards, slots, tile, rank), 'shard', spli...  132 us
    all_gather x1, blocking collectives, per_device(): gram = jnp.sum(all_gather(local_gram, axis_name='shard'), axis=0)  85.2 us
    psum x1, waiting for transfers between devices, per_device(): total = lax.psum(owner_sum, 'rep')  83.7 us
    dot_general x3, matrix products, apply_system(): jnp.einsum('bktl,bklr->btr', weighted, fetched, preferred_element_type=jn...  14.5 us
    all_to_all x1, blocking collectives, per_device(): lax.all_to_all(requests, 'shard', split_axis=0, concat_axis=0, tiled=True)  13.6 us
    dot_general x1, matrix products, per_device(): jnp.dot(selector, returned.reshape(shards * slots, tile * rank), precisio...  10.8 us
  transfers between devices with their start and end apart: 3, of which 2 were waited for; matrix products, arithmetic and copies ran while one was open for 2% of the time, Pallas kernels for 0%

profile of v1, /device:TPU:0, one launch (start us, length us, event | category | flops | bytes accessed | tf_op | source)
XLA Modules:
  0.0 418.2 jit_solution(11923799878584432541)
XLA Ops:
  7.2 0.0 copy-start
  7.2 0.9 reshape.224
  8.1 0.8 reshape.223
  8.9 0.1 fusion.50
  9.0 0.2 select_reduce_fusion
  9.2 0.6 scatter_custom_fusion
  9.8 0.1 all_to_all.14
  9.9 13.6 %all_to_all.22 = s32[8,1,6]{2,1,0:T(1,128)S(1)} all-to-all(s32[8,1,6]{2,1,0:T(1,128)S(1)} %bitcast.114), channel_id=1, replica_groups=mesh['shard'=8,'rep'=4] {'shard'}, dimensions={0} | all-to-all | bytes 384 | tf_op jit(solution)/shard_map/all_to_all | solution.py:45
  23.5 0.1 copy.34
  23.6 0.1 copy.35
  23.7 0.1 reshape.233
  23.8 0.0 copy-done
  23.8 2.7 gather_fusion
  26.5 4.4 %all-to-all-start.1 = ((bf16[8,6,256,128]{3,2,1,0:T(8,128)(2,1)}), bf16[8,6,256,128]{3,2,1,0:T(8,128)(2,1)}, u32[]{:S(2)}, u32[]{:S(2)}) async-start(bf16[8,6,256,128]{3,2,1,0:T(8,128)(2,1)} %bitcast.107), calls=%async_computation.1 | async-start | bytes 6291456 | tf_op jit(solution)/shard_map/all_to_all | solution.py:46
  30.9 4.7 %copy.39 = bf16[3,8,256,256]{2,3,1,0:T(8,128)(2,1)} copy(bf16[3,8,256,256]{3,2,1,0:T(8,128)(2,1)} %param.4) | data formatting | bytes 6291456 | tf_op args[1]
  35.6 0.7 fusion.55
  36.4 85.2 %all-gather = f32[1024,128]{1,0:T(8,128)S(1)} all-gather(f32[128,128]{1,0:T(8,128)S(1)} %fusion.55), channel_id=2, replica_groups=mesh['shard'=8,'rep'=4] {'shard'}, dimensions={0}, use_global_device_ids=true | all-gather | bytes 589824 | tf_op jit(solution)/shard_map/all_gather | solution.py:34
  121.6 0.0 all-to-all-done.1
  121.6 3.8 gather_fusion.1
  125.4 3.5 convolution_bitcast_fusion
  129.0 4.3 %fusion.18 = f32[3,256,128]{1,2,0:T(8,128)S(1)} fusion(bf16[3,8,256,128]{3,2,1,0:T(8,128)(2,1)} %bitcast.109, bf16[3,8,256,256]{2,3,1,0:T(8,128)(2,1)} %copy.39, f32[3,256,128]{1,2,0:T(8,128)S(1)} %convolution_bitcast_fusion), kind=kOutput, calls=%fused_computation.20 | convolution fusion | flops 810123264 | bytes 5505024 | tf_op jit(solution)/shard_map/bktl,bklr->btr/dot_general | solution.py:15
  133.3 0.6 multiply_reduce_fusion.3
  133.9 0.1 multiply_reduce_fusion.2
  134.0 0.1 multiply_add_fusion.2
  134.0 5.0 %fusion.21 = f32[3,256,128]{1,2,0:T(8,128)} fusion(bf16[3,8,256,128]{3,2,1,0:T(8,128)(2,1)} %bitcast.110, bf16[3,8,256,256]{2,3,1,0:T(8,128)(2,1)} %copy.39, f32[3,256,128]{1,2,0:T(8,128)S(1)} %multiply_add_fusion.2), kind=kOutput, calls=%fused_computation.21 | convolution fusion | flops 810123264 | bytes 5505024 | tf_op jit(solution)/shard_map/bktl,bklr->btr/dot_general | solution.py:15
  139.1 1.6 multiply_reduce_fusion.1
  140.7 0.1 multiply_reduce_fusion
  140.7 0.8 multiply_add_fusion.1
  141.6 5.2 %fusion.24 = f32[3,256,128]{1,2,0:T(8,128)} fusion(bf16[3,8,256,128]{3,2,1,0:T(8,128)(2,1)} %bitcast.111, bf16[3,8,256,256]{2,3,1,0:T(8,128)(2,1)} %copy.39, f32[3,256,128]{1,2,0:T(8,128)} %multiply_add_fusion.1), kind=kOutput, calls=%fused_computation.22 | convolution fusion | flops 810123264 | bytes 5505024 | tf_op jit(solution)/shard_map/bktl,bklr->btr/dot_general | solution.py:15
  146.8 0.0 copy-done.1
  146.8 1.6 fusion.31
  148.3 1.1 multiply_add_fusion
  149.4 4.1 fusion.38
  153.6 3.6 copy.54
  157.2 3.4 broadcast_in_dim.5
  160.6 7.9 %scatter_fusion = f32[48,256,128]{2,1,0:T(8,128)} fusion(f32[48,256,128]{2,1,0:T(8,128)} %broadcast_in_dim.5, s32[24]{0:T(128)S(1)} %fusion.52, f32[24,256,128]{2,1,0:T(8,128)} %copy.54), kind=kCustom, calls=%fused_computation.3 | custom fusion | bytes 9437280 | tf_op jit(solution)/shard_map/scatter | solution.py:70
  168.5 4.8 %all-to-all-start.2 = ((f32[8,6,256,128]{3,2,1,0:T(8,128)}), f32[8,6,256,128]{3,2,1,0:T(8,128)}, u32[]{:S(2)}, u32[]{:S(2)}) async-start(f32[8,6,256,128]{3,2,1,0:T(8,128)} %bitcast.105), calls=%async_computation.2 | async-start | bytes 12582912 | tf_op jit(solution)/shard_map/all_to_all | solution.py:72
  173.3 0.2 all-reduce.2.cloned.1.call-start
  173.5 0.5 broadcast.206
  174.0 0.7 reduce.3
  174.7 0.1 eq.31
  174.7 131.8 %all-to-all-done.2 = f32[8,6,256,128]{3,2,1,0:T(8,128)} async-done(((f32[8,6,256,128]{3,2,1,0:T(8,128)}), f32[8,6,256,128]{3,2,1,0:T(8,128)}, u32[]{:S(2)}, u32[]{:S(2)}) %all-to-all-start.2) | async-done | bytes 6291488 | tf_op jit(solution)/shard_map/all_to_all | solution.py:72
  306.5 10.8 %fusion.3 = f32[32,32768]{1,0:T(8,128)} fusion(f32[6,8,256,128]{3,2,1,0:T(8,128)} %bitcast.41, s32[48]{0:T(128)S(1)} %eq.31), kind=kOutput, calls=%fused_computation.10 | convolution fusion | flops 603981312 | bytes 10485952 | tf_op jit(solution)/shard_map/dot_general | solution.py:82
  317.4 0.0 all-reduce.2.cloned.1.call-update
  317.4 0.9 copy.53
  318.3 83.7 %all-reduce.2.cloned.1.call-done = f32[32,32768]{1,0:T(8,128)} async-done(((f32[32,32768]{1,0:T(8,128)}), f32[32,32768]{1,0:T(8,128)}) %all-reduce.2.cloned.1.call-update) | async-done | bytes 4194320 | tf_op jit(solution)/shard_map/psum | solution.py:88
  402.0 4.4 %broadcast_multiply_fusion = f32[32,32768]{1,0:T(8,128)} fusion(f32[32,32768]{1,0:T(8,128)} %all-reduce.2.cloned.1.call-done), kind=kLoop, calls=%fused_computation.19 | loop fusion | flops 1048576 | bytes 8388608 | tf_op jit(solution)/shard_map/div | solution.py:90
  406.5 4.9 %div.83 = f32[8192,128]{1,0:T(8,128)} reshape(f32[32,32768]{1,0:T(8,128)} %broadcast_multiply_fusion) | data formatting | bytes 8388608 | tf_op jit(solution)/shard_map/div | solution.py:90
  (13 shorter events, 0.2 us)
Async XLA Ops:
  7.2 16.6 %copy-start = (bf16[8192,128]{1,0:T(8,128)(2,1)S(1)}, bf16[8192,128]{1,0:T(8,128)(2,1)}, u32[]{:S(2)}) copy-start(bf16[8192,128]{1,0:T(8,128)(2,1)} %param.5) | copy-start | bytes 6291460
  26.5 95.1 %all-to-all-start.1 = ((bf16[8,6,256,128]{3,2,1,0:T(8,128)(2,1)}), bf16[8,6,256,128]{3,2,1,0:T(8,128)(2,1)}, u32[]{:S(2)}, u32[]{:S(2)}) async-start(bf16[8,6,256,128]{3,2,1,0:T(8,128)(2,1)} %bitcast.107), calls=%async_computation.1 | async-start | bytes 6291456 | tf_op jit(solution)/shard_map/all_to_all | solution.py:46
  141.6 5.2 %copy-start.1 = (f32[3,256,128]{1,2,0:T(8,128)S(1)}, f32[3,256,128]{1,2,0:T(8,128)}, u32[]{:S(2)}) copy-start(f32[3,256,128]{1,2,0:T(8,128)} %multiply_add_fusion.1) | copy-start | bytes 1179652
  168.5 138.0 %all-to-all-start.2 = ((f32[8,6,256,128]{3,2,1,0:T(8,128)}), f32[8,6,256,128]{3,2,1,0:T(8,128)}, u32[]{:S(2)}, u32[]{:S(2)}) async-start(f32[8,6,256,128]{3,2,1,0:T(8,128)} %bitcast.105), calls=%async_computation.2 | async-start | bytes 12582912 | tf_op jit(solution)/shard_map/all_to_all | solution.py:72
  173.3 228.8 %all-reduce.2.cloned.1.call-start = ((), (), s32[]{:S(2)}) async-start(), calls=%async_computation.3 | async-start | bytes 8388608 | tf_op jit(solution)/shard_map/psum | solution.py:88
Sparse Core Ops, SparseCore 0:
  317.5 84.4 all-reduce.1
